TPU v7x, 32 devices: a whole 2x2x4 slice. The times are simulated.
32 devices in a mesh: gx: 4 (over z), gy: 4 (over y, core), gz: 2 (over x).
Axes of the slice: x: 2, y: 2, z: 4, core: 2. Of those that a mesh axis runs over, the one named last changes fastest.
Arguments:
- right_side: float32 [128, 128, 256], P('gx', 'gy', 'gz'), may hold values from -8 to 8
- guess: float32 [128, 128, 256], P('gx', 'gy', 'gz'), may hold values from -4 to 4
Outputs:
- solution_field: float32 [128, 128, 256], P('gx', 'gy', 'gz')
- residual: float32 [128, 128, 256], P('gx', 'gy', 'gz')
All inputs are finite; a program needn't handle non-finite values.
Results may differ from a plain program's by a relative error of at most 0.0001.
Values sent between devices are 32-bit elements; how exact they have to be, the bound alone decides.
A program may use at most 128 MiB of HBM per device.

v0:
```python
import jax
import jax.numpy as jnp
from jax import lax
from jax.sharding import PartitionSpec as P

LEVELS = 6
SWEEPS = 4
STEPS = 2
damping = 2.0 / 3.0


def passed_along(value, axis, steps):
    count = lax.axis_size(axis)
    first, last = (max(0, -steps), min(count, count - steps))
    return lax.ppermute(value, axis, [(source, source + steps) for source in range(first, last)])


def padded_2(x, sides, width):
    for axis, dim in sides:
        count, length = (lax.axis_size(axis), x.shape[dim])
        up = [(i, (i + 1) % count) for i in range(count - 1)]
        down = [(j, i) for i, j in up]
        last = lax.slice_in_dim(x, length - width, length, axis=dim)
        first = lax.slice_in_dim(x, 0, width, axis=dim)
        before = lax.ppermute(last, axis, up)
        after = lax.ppermute(first, axis, down)
        x = jnp.concatenate([before, x, after], axis=dim)
    return x


def padded_stencil(padded):
    beside = padded[2:, 1:-1, 1:-1] + padded[:-2, 1:-1, 1:-1]
    beside = beside + padded[1:-1, 2:, 1:-1] + padded[1:-1, :-2, 1:-1]
    beside = beside + padded[1:-1, 1:-1, 2:] + padded[1:-1, 1:-1, :-2]
    return 6.0 * padded[1:-1, 1:-1, 1:-1] - beside


def restrict(field):
    first, second, third = field.shape
    blocks = field.reshape(first // 2, 2, second // 2, 2, third // 2, 2)
    return jnp.mean(blocks, axis=(1, 3, 5))


def prolong(field):
    first, second, third = field.shape
    spread = jnp.broadcast_to(field[:, None, :, None, :, None], (first, 2, second, 2, third, 2))
    return spread.reshape(first * 2, second * 2, third * 2)


def axis_layers(packed, axis_name, by):
    if axis_name == "gx":
        return passed_along(packed, "gx", by)
    if axis_name == "gy":
        return passed_along(packed, "gy", by)
    return passed_along(packed, "gz", by)


def extend_all(fields, margin):
    current = list(fields)
    for dim_index, axis_name in ((0, "gx"), (1, "gy"), (2, "gz")):
        lows = [lax.slice_in_dim(f, 0, margin, axis=dim_index) for f in current]
        highs = [
            lax.slice_in_dim(f, f.shape[dim_index] - margin, f.shape[dim_index], axis=dim_index)
            for f in current
        ]
        received = {}
        for by in (1, -1):
            pieces = highs if by == 1 else lows
            packed = jnp.concatenate([p.reshape(-1) for p in pieces])
            received[by] = axis_layers(packed, axis_name, by)
        grown = []
        offset = 0
        for index, field in enumerate(current):
            piece_shape = lows[index].shape
            count = lows[index].size
            from_lower = received[1][offset : offset + count].reshape(piece_shape)
            from_upper = received[-1][offset : offset + count].reshape(piece_shape)
            offset = offset + count
            grown.append(jnp.concatenate([from_lower, field, from_upper], axis=dim_index))
        current = grown
    return current


def smooth_merged(items):
    results = {}
    approxes = [damping * rhs / (6.0 * 0.25**lev) for rhs, lev in items]
    for sweep_index in range(SWEEPS - 1):
        padded_list = extend_all(approxes, 1)
        renewed = []
        for index, (rhs, lev) in enumerate(items):
            scaling = 0.25**lev
            diagonal_value = 6.0 * scaling
            renewed.append(
                approxes[index]
                + damping * (rhs - scaling * padded_stencil(padded_list[index])) / diagonal_value
            )
        approxes = renewed
    for index, (rhs, lev) in enumerate(items):
        results[lev] = approxes[index]
    return results


def precondition(residual):
    chain = [residual]
    for level_index in range(1, LEVELS):
        chain.append(restrict(chain[-1]))
    first_level = LEVELS - 1
    local_levels = list(range(first_level + 1))
    smoothed = smooth_merged([(chain[lev], lev) for lev in local_levels])
    correction = smoothed[first_level]
    for level_index in range(first_level - 1, -1, -1):
        correction = prolong(correction) + smoothed[level_index]
    return correction


def apply_fine(field):
    padded = padded_2(field, (("gx", 0), ("gy", 1), ("gz", 2)), 1)
    return padded_stencil(padded)


def shards(right_side, guess):
    solution_field = guess
    residual = right_side - apply_fine(guess)
    for step_index in range(STEPS):
        direction = precondition(residual)
        image = apply_fine(direction)
        along, curvature = lax.psum(
            (jnp.sum(residual * direction), jnp.sum(direction * image)), ("gx", "gy", "gz")
        )
        alpha = along / curvature
        solution_field = solution_field + alpha * direction
        residual = residual - alpha * image
    return (solution_field, residual)


def solution(mesh):
    placed = (P("gx", "gy", "gz"), P("gx", "gy", "gz"))
    return jax.shard_map(
        shards,
        mesh=mesh,
        in_specs=placed,
        out_specs=(P("gx", "gy", "gz"), P("gx", "gy", "gz")),
        check_vma=False,
    )
```

profile of v0, /device:TPU:0, one launch (start us, length us, event | category | flops | bytes accessed | tf_op | source)
XLA Modules:
  0.0 606.6 jit_solution(4249604036732145625)
XLA Ops:
  2.7 5.6 collective-permute-start.1
  17.2 4.5 collective-permute-start.5
  25.7 34.9 %reshape.1638 = f32[16,2,16,2,64,2]{5,4,3,2,1,0:T(8,128)} reshape(f32[32,32,128]{2,1,0:T(8,128)S(1)} %copy.405) | data formatting | bytes 1048576 | tf_op jit(solution)/shard_map/reshape | solution.py:40
  60.5 12.2 %reduce_sum.140 = f32[16,16,64]{2,1,0:T(8,128)S(1)} reduce(f32[16,2,16,2,64,2]{5,4,3,2,1,0:T(8,128)} %reshape.1638, f32[]{:T(128)} %constant.169.clone.1), dimensions={1,3,5}, to_apply=%region_0.0 | reduce | flops 114688 | bytes 589828 | tf_op jit(solution)/shard_map/reduce_sum | solution.py:41
  72.8 5.6 div.223
  97.4 5.7 collective-permute-done.8
  109.0 4.7 collective-permute-start.11
  190.2 4.9 collective-permute-start.23
  204.2 4.9 reshape.1846
  210.7 11.4 %broadcast_in_dim.39 = f32[16,2,16,2,64,2]{5,4,3,2,1,0:T(8,128)} broadcast(f32[16,16,64]{2,1,0:T(8,128)S(1)} %fusion.112), dimensions={0,2,4} | broadcast | bytes 589824 | tf_op jit(solution)/shard_map/broadcast_in_dim | solution.py:46
  222.0 24.1 %reshape.1849 = f32[32,32,128]{2,1,0:T(8,128)S(1)} reshape(f32[16,2,16,2,64,2]{5,4,3,2,1,0:T(8,128)} %broadcast_in_dim.39) | data formatting | bytes 1048576 | tf_op jit(solution)/shard_map/reshape | solution.py:47
  250.0 4.5 collective-permute-start.25
  263.5 4.5 collective-permute-start.29
  271.1 45.0 %all-reduce.1 = (f32[]{:T(128)}, f32[]{:T(128)}) all-reduce(f32[]{:T(128)} %get-tuple-element.9, f32[]{:T(128)} %get-tuple-element.8), channel_id=1, replica_groups=mesh['gx'=4,'gy'=4,'gz'=2] {'gx','gy','gz'}, use_global_device_ids=true, to_apply=%region_7.0 | all-reduce | flops 2 | bytes 16 | tf_op jit(solution)/shard_map/psum | solution.py:127
  317.9 34.9 %reshape.1852 = f32[16,2,16,2,64,2]{5,4,3,2,1,0:T(8,128)} reshape(f32[32,32,128]{2,1,0:T(8,128)S(1)} %copy.511) | data formatting | bytes 1048576 | tf_op jit(solution)/shard_map/reshape | solution.py:40
  352.7 12.2 %reduce_sum.149 = f32[16,16,64]{2,1,0:T(8,128)S(1)} reduce(f32[16,2,16,2,64,2]{5,4,3,2,1,0:T(8,128)} %reshape.1852, f32[]{:T(128)} %constant.169.clone.1), dimensions={1,3,5}, to_apply=%region_10.0 | reduce | flops 114688 | bytes 589828 | tf_op jit(solution)/shard_map/reduce_sum | solution.py:41
  365.0 5.6 div.269
  477.2 4.8 collective-permute-start.47
  488.1 4.9 reshape.2060
  493.8 11.4 %broadcast_in_dim.87 = f32[16,2,16,2,64,2]{5,4,3,2,1,0:T(8,128)} broadcast(f32[16,16,64]{2,1,0:T(8,128)S(1)} %fusion.81), dimensions={0,2,4} | broadcast | bytes 589824 | tf_op jit(solution)/shard_map/broadcast_in_dim | solution.py:46
  505.1 24.5 %reshape.2063 = f32[32,32,128]{2,1,0:T(8,128)} reshape(f32[16,2,16,2,64,2]{5,4,3,2,1,0:T(8,128)} %broadcast_in_dim.87) | data formatting | bytes 1048576 | tf_op jit(solution)/shard_map/reshape | solution.py:47
  533.8 4.5 collective-permute-start.49
  547.9 4.5 collective-permute-start.53
  556.4 44.8 %all-reduce = (f32[]{:T(128)}, f32[]{:T(128)}) all-reduce(f32[]{:T(128)} %get-tuple-element.7, f32[]{:T(128)} %get-tuple-element.6), channel_id=1, replica_groups=mesh['gx'=4,'gy'=4,'gz'=2] {'gx','gy','gz'}, use_global_device_ids=true, to_apply=%region_17.0 | all-reduce | flops 2 | bytes 16 | tf_op jit(solution)/shard_map/psum | solution.py:127
  (1048 shorter events, 275.5 us)
Async XLA Ops:
  1.4 8.2 %collective-permute-start = (f32[1,32,128]{2,0,1:T(1,128)S(1)}, f32[1,32,128]{2,0,1:T(1,128)S(1)}, u32[]{:S(2)}, u32[]{:S(2)}) collective-permute-start(f32[1,32,128]{2,0,1:T(1,128)S(1)} %bitcast.399), channel_id=1, source_target_pairs={{8,0},{16,8},{24,16},{9,1},{17,9},{25,17},{10,2},{18,10},{26,18},{... | collective-permute-start | bytes 49160 | tf_op jit(solution)/shard_map/ppermute | solution.py:26
  2.7 7.0 %collective-permute-start.1 = (f32[1,32,128]{2,0,1:T(1,128)S(1)}, f32[1,32,128]{2,0,1:T(1,128)S(1)}, u32[]{:S(2)}, u32[]{:S(2)}) collective-permute-start(f32[1,32,128]{2,0,1:T(1,128)S(1)} %bitcast.398), channel_id=1, source_target_pairs={{0,8},{8,16},{16,24},{1,9},{9,17},{17,25},{2,10},{10,18},{18,26},{... | collective-permute-start | bytes 49160 | tf_op jit(solution)/shard_map/ppermute | solution.py:25
  15.5 6.2 %collective-permute-start.4 = (f32[34,34,1]{1,2,0:T(1,128)S(1)}, f32[34,34,1]{1,2,0:T(1,128)S(1)}, u32[]{:S(2)}, u32[]{:S(2)}) collective-permute-start(f32[34,34,1]{1,2,0:T(1,128)S(1)} %copy.400), channel_id=1, source_target_pairs={{1,0},{3,2},{5,4},{7,6},{9,8},{11,10},{13,12},{15,14},{17,16},{19,... | collective-permute-start | bytes 13880 | tf_op jit(solution)/shard_map/ppermute | solution.py:26
  17.2 6.0 collective-permute-start.5
  82.3 5.9 collective-permute-start.7
  95.9 7.1 %collective-permute-start.8 = (f32[5964]{0:T(1024)S(1)}, f32[5964]{0:T(1024)S(1)}, u32[]{:S(2)}, u32[]{:S(2)}) collective-permute-start(f32[5964]{0:T(1024)S(1)} %concatenate.1027), channel_id=1, source_target_pairs={{2,0},{4,2},{6,4},{3,1},{5,3},{7,5},{10,8},{12,10},{14,12},{11,9},... | collective-permute-start | bytes 71576 | tf_op jit(solution)/shard_map/ppermute | solution.py:15
  106.6 7.2 %collective-permute-start.10 = (f32[1641]{0:T(1024)S(1)}, f32[1641]{0:T(1024)S(1)}, u32[]{:S(2)}, u32[]{:S(2)}) collective-permute-start(f32[1641]{0:T(1024)S(1)} %concatenate.1035), channel_id=1, source_target_pairs={{1,0},{3,2},{5,4},{7,6},{9,8},{11,10},{13,12},{15,14},{17,16},{19,... | collective-permute-start | bytes 19700 | tf_op jit(solution)/shard_map/ppermute | solution.py:15
  109.0 5.9 collective-permute-start.11
  145.3 7.0 %collective-permute-start.16 = (f32[1641]{0:T(1024)S(1)}, f32[1641]{0:T(1024)S(1)}, u32[]{:S(2)}, u32[]{:S(2)}) collective-permute-start(f32[1641]{0:T(1024)S(1)} %concatenate.1085), channel_id=1, source_target_pairs={{1,0},{3,2},{5,4},{7,6},{9,8},{11,10},{13,12},{15,14},{17,16},{19,... | collective-permute-start | bytes 19700 | tf_op jit(solution)/shard_map/ppermute | solution.py:15
  147.7 5.9 collective-permute-start.17
  163.2 7.2 %collective-permute-start.19 = (f32[5460]{0:T(1024)S(1)}, f32[5460]{0:T(1024)S(1)}, u32[]{:S(2)}, u32[]{:S(2)}) collective-permute-start(f32[5460]{0:T(1024)S(1)} %concatenate.1120), channel_id=1, source_target_pairs={{0,8},{8,16},{16,24},{1,9},{9,17},{17,25},{2,10},{10,18},{18,26},{... | collective-permute-start | bytes 65528 | tf_op jit(solution)/shard_map/ppermute | solution.py:15
  187.7 7.4 %collective-permute-start.22 = (f32[1641]{0:T(1024)S(1)}, f32[1641]{0:T(1024)S(1)}, u32[]{:S(2)}, u32[]{:S(2)}) collective-permute-start(f32[1641]{0:T(1024)S(1)} %concatenate.1135), channel_id=1, source_target_pairs={{1,0},{3,2},{5,4},{7,6},{9,8},{11,10},{13,12},{15,14},{17,16},{19,... | collective-permute-start | bytes 19700 | tf_op jit(solution)/shard_map/ppermute | solution.py:15
  190.2 5.9 collective-permute-start.23
  250.0 6.0 collective-permute-start.25
  261.8 6.2 %collective-permute-start.28 = (f32[34,34,1]{1,2,0:T(1,128)S(1)}, f32[34,34,1]{1,2,0:T(1,128)S(1)}, u32[]{:S(2)}, u32[]{:S(2)}) collective-permute-start(f32[34,34,1]{1,2,0:T(1,128)S(1)} %copy.506), channel_id=1, source_target_pairs={{1,0},{3,2},{5,4},{7,6},{9,8},{11,10},{13,12},{15,14},{17,16},{19,... | collective-permute-start | bytes 13880 | tf_op jit(solution)/shard_map/ppermute | solution.py:26
  263.5 6.0 collective-permute-start.29
  397.0 7.0 %collective-permute-start.34 = (f32[1641]{0:T(1024)S(1)}, f32[1641]{0:T(1024)S(1)}, u32[]{:S(2)}, u32[]{:S(2)}) collective-permute-start(f32[1641]{0:T(1024)S(1)} %concatenate.1193), channel_id=1, source_target_pairs={{1,0},{3,2},{5,4},{7,6},{9,8},{11,10},{13,12},{15,14},{17,16},{19,... | collective-permute-start | bytes 19700 | tf_op jit(solution)/shard_map/ppermute | solution.py:15
  399.4 5.9 collective-permute-start.35
  435.2 7.0 %collective-permute-start.40 = (f32[1641]{0:T(1024)S(1)}, f32[1641]{0:T(1024)S(1)}, u32[]{:S(2)}, u32[]{:S(2)}) collective-permute-start(f32[1641]{0:T(1024)S(1)} %concatenate.1243), channel_id=1, source_target_pairs={{1,0},{3,2},{5,4},{7,6},{9,8},{11,10},{13,12},{15,14},{17,16},{19,... | collective-permute-start | bytes 19700 | tf_op jit(solution)/shard_map/ppermute | solution.py:15
  437.6 5.9 collective-permute-start.41
  474.8 7.2 %collective-permute-start.46 = (f32[1641]{0:T(1024)S(1)}, f32[1641]{0:T(1024)S(1)}, u32[]{:S(2)}, u32[]{:S(2)}) collective-permute-start(f32[1641]{0:T(1024)S(1)} %concatenate.1293), channel_id=1, source_target_pairs={{1,0},{3,2},{5,4},{7,6},{9,8},{11,10},{13,12},{15,14},{17,16},{19,... | collective-permute-start | bytes 19700 | tf_op jit(solution)/shard_map/ppermute | solution.py:15
  533.8 6.0 collective-permute-start.49
  546.2 6.2 %collective-permute-start.52 = (f32[34,34,1]{1,2,0:T(1,128)S(1)}, f32[34,34,1]{1,2,0:T(1,128)S(1)}, u32[]{:S(2)}, u32[]{:S(2)}) collective-permute-start(f32[34,34,1]{1,2,0:T(1,128)S(1)} %copy.612), channel_id=1, source_target_pairs={{1,0},{3,2},{5,4},{7,6},{9,8},{11,10},{13,12},{15,14},{17,16},{19,... | collective-permute-start | bytes 13880 | tf_op jit(solution)/shard_map/ppermute | solution.py:26
  547.9 6.0 collective-permute-start.53
  (55 other events, 590.3 us)
where the time goes:
time: 617 us; the launch traced here: 607 us
  local copies, waits for them, and re-layouts  258 us (42%)
  starting transfers between devices  131 us (21%)
  blocking collectives  89.7 us (15%)
  waiting for transfers between devices  64.4 us (10%)
  other arithmetic  57.4 us (9%)
  between operations  6.56 us (1%)
    psum x2, blocking collectives, shards(): lax.psum((jnp.sum(residual * direction), jnp.sum(direction * image)), ('g...  89.7 us
    ppermute x36, starting transfers between devices, passed_along(): lax.ppermute(value, axis, [(source, source + steps) for source in range(f...  81.6 us
    reshape x2, local copies, waits for them, and re-layouts, restrict(): blocks = field.reshape(first // 2, 2, second // 2, 2, third // 2, 2)  69.7 us
    reshape x8, local copies, waits for them, and re-layouts, prolong(): return spread.reshape(first * 2, second * 2, third * 2)  58.9 us
    ppermute x36, waiting for transfers between devices, passed_along(): lax.ppermute(value, axis, [(source, source + steps) for source in range(f...  56 us
    ppermute x9, starting transfers between devices, padded_2(): before = lax.ppermute(last, axis, up)  37.4 us
    reduce_sum x12, other arithmetic, restrict(): return jnp.mean(blocks, axis=(1, 3, 5))  30.3 us
    broadcast_in_dim x12, local copies, waits for them, and re-layouts, prolong(): jnp.broadcast_to(field[:, None, :, None, :, None], (first, 2, second, 2,...  28.4 us
  transfers between devices with their start and end apart: 54, of which 27 were waited for; matrix products, arithmetic and copies ran while one was open for 3% of the time, Pallas kernels for 0%

commit v1 on v0

--- a/solution.py
+++ b/solution.py
@@ -125,7 +125,8 @@
         direction = precondition(residual)
         image = apply_fine(direction)
         along, curvature = lax.psum(
-            (jnp.sum(residual * direction), jnp.sum(direction * image)), ("gx", "gy", "gz")
+            lax.psum((jnp.sum(residual * direction), jnp.sum(direction * image)), ("gy", "gz")),
+            "gx",
         )
         alpha = along / curvature
         solution_field = solution_field + alpha * direction

time: 617 us -> 582 us (0.943)
  blocking collectives: 89.7 us -> 56.8 us
    psum x2, blocking collectives: 89.7 us -> 34 us  [shards(): lax.psum((jnp.sum(residual * direction), jnp.sum(direction * image)), ('g...]
    psum x0 -> x2, blocking collectives: none -> 22.7 us  [shards(): lax.psum(lax.psum((jnp.sum(residual * direction), jnp.sum(direction * ima...]
where the time goes in v1:
time: 582 us; the launch traced here: 572 us
  local copies, waits for them, and re-layouts  258 us (44%)
  starting transfers between devices  128 us (22%)
  waiting for transfers between devices  64.6 us (11%)
  other arithmetic  57.4 us (10%)
  blocking collectives  56.8 us (10%)
  between operations  6.5 us (1%)
    ppermute x36, starting transfers between devices, passed_along(): lax.ppermute(value, axis, [(source, source + steps) for source in range(f...  79.4 us
    reshape x2, local copies, waits for them, and re-layouts, restrict(): blocks = field.reshape(first // 2, 2, second // 2, 2, third // 2, 2)  69.7 us
    reshape x8, local copies, waits for them, and re-layouts, prolong(): return spread.reshape(first * 2, second * 2, third * 2)  58.9 us
    ppermute x36, waiting for transfers between devices, passed_along(): lax.ppermute(value, axis, [(source, source + steps) for source in range(f...  56.2 us
    ppermute x9, starting transfers between devices, padded_2(): before = lax.ppermute(last, axis, up)  37.4 us
    psum x2, blocking collectives, shards(): lax.psum((jnp.sum(residual * direction), jnp.sum(direction * image)), ('g...  34 us
    reduce_sum x12, other arithmetic, restrict(): return jnp.mean(blocks, axis=(1, 3, 5))  30.3 us
    broadcast_in_dim x12, local copies, waits for them, and re-layouts, prolong(): jnp.broadcast_to(field[:, None, :, None, :, None], (first, 2, second, 2,...  28.4 us
  transfers between devices with their start and end apart: 54, of which 27 were waited for; matrix products, arithmetic and copies ran while one was open for 3% of the time, Pallas kernels for 0%

profile of v1, /device:TPU:0, one launch (start us, length us, event | category | flops | bytes accessed | tf_op | source)
XLA Modules:
  0.0 571.6 jit_solution(18115075936510995777)
XLA Ops:
  2.7 5.6 collective-permute-start.1
  17.2 4.5 collective-permute-start.5
  25.7 34.9 %reshape.1638 = f32[16,2,16,2,64,2]{5,4,3,2,1,0:T(8,128)} reshape(f32[32,32,128]{2,1,0:T(8,128)S(1)} %copy.405) | data formatting | bytes 1048576 | tf_op jit(solution)/shard_map/reshape | solution.py:40
  60.5 12.2 %reduce_sum.140 = f32[16,16,64]{2,1,0:T(8,128)S(1)} reduce(f32[16,2,16,2,64,2]{5,4,3,2,1,0:T(8,128)} %reshape.1638, f32[]{:T(128)} %constant.169.clone.1), dimensions={1,3,5}, to_apply=%region_0.0 | reduce | flops 114688 | bytes 589828 | tf_op jit(solution)/shard_map/reduce_sum | solution.py:41
  72.8 5.6 div.223
  97.4 5.7 collective-permute-done.8
  109.0 4.7 collective-permute-start.11
  190.2 4.9 collective-permute-start.23
  204.2 4.9 reshape.1846
  210.7 11.4 %broadcast_in_dim.39 = f32[16,2,16,2,64,2]{5,4,3,2,1,0:T(8,128)} broadcast(f32[16,16,64]{2,1,0:T(8,128)S(1)} %fusion.112), dimensions={0,2,4} | broadcast | bytes 589824 | tf_op jit(solution)/shard_map/broadcast_in_dim | solution.py:46
  222.0 24.1 %reshape.1849 = f32[32,32,128]{2,1,0:T(8,128)S(1)} reshape(f32[16,2,16,2,64,2]{5,4,3,2,1,0:T(8,128)} %broadcast_in_dim.39) | data formatting | bytes 1048576 | tf_op jit(solution)/shard_map/reshape | solution.py:47
  250.0 4.5 collective-permute-start.25
  263.5 4.5 collective-permute-start.29
  271.1 17.0 %all-reduce.1 = (f32[]{:T(128)}, f32[]{:T(128)}) all-reduce(f32[]{:T(128)} %get-tuple-element.9, f32[]{:T(128)} %get-tuple-element.8), channel_id=1, replica_groups=mesh['gx'=4,'gy'=4,'gz'=2] {'gy','gz'}, use_global_device_ids=true, to_apply=%region_7.0 | all-reduce | flops 2 | bytes 16 | tf_op jit(solution)/shard_map/psum | solution.py:128
  288.2 11.4 %all-reduce.3 = (f32[]{:T(128)}, f32[]{:T(128)}) all-reduce(f32[]{:T(128)} %get-tuple-element.96, f32[]{:T(128)} %get-tuple-element.97), channel_id=1, replica_groups=mesh['gx'=4,'gy'=4,'gz'=2] {'gx'}, use_global_device_ids=true, to_apply=%region_8.0 | all-reduce | flops 2 | bytes 16 | tf_op jit(solution)/shard_map/psum | solution.py:127
  301.4 34.9 %reshape.1852 = f32[16,2,16,2,64,2]{5,4,3,2,1,0:T(8,128)} reshape(f32[32,32,128]{2,1,0:T(8,128)S(1)} %copy.511) | data formatting | bytes 1048576 | tf_op jit(solution)/shard_map/reshape | solution.py:40
  336.3 12.2 %reduce_sum.149 = f32[16,16,64]{2,1,0:T(8,128)S(1)} reduce(f32[16,2,16,2,64,2]{5,4,3,2,1,0:T(8,128)} %reshape.1852, f32[]{:T(128)} %constant.169.clone.1), dimensions={1,3,5}, to_apply=%region_12.0 | reduce | flops 114688 | bytes 589828 | tf_op jit(solution)/shard_map/reduce_sum | solution.py:41
  348.5 5.6 div.269
  469.6 4.9 reshape.2060
  475.3 11.4 %broadcast_in_dim.87 = f32[16,2,16,2,64,2]{5,4,3,2,1,0:T(8,128)} broadcast(f32[16,16,64]{2,1,0:T(8,128)S(1)} %fusion.81), dimensions={0,2,4} | broadcast | bytes 589824 | tf_op jit(solution)/shard_map/broadcast_in_dim | solution.py:46
  486.7 24.5 %reshape.2063 = f32[32,32,128]{2,1,0:T(8,128)} reshape(f32[16,2,16,2,64,2]{5,4,3,2,1,0:T(8,128)} %broadcast_in_dim.87) | data formatting | bytes 1048576 | tf_op jit(solution)/shard_map/reshape | solution.py:47
  515.3 4.5 collective-permute-start.49
  537.9 17.0 %all-reduce = (f32[]{:T(128)}, f32[]{:T(128)}) all-reduce(f32[]{:T(128)} %get-tuple-element.7, f32[]{:T(128)} %get-tuple-element.6), channel_id=1, replica_groups=mesh['gx'=4,'gy'=4,'gz'=2] {'gy','gz'}, use_global_device_ids=true, to_apply=%region_19.0 | all-reduce | flops 2 | bytes 16 | tf_op jit(solution)/shard_map/psum | solution.py:128
  554.9 11.3 %all-reduce.2 = (f32[]{:T(128)}, f32[]{:T(128)}) all-reduce(f32[]{:T(128)} %get-tuple-element.94, f32[]{:T(128)} %get-tuple-element.95), channel_id=1, replica_groups=mesh['gx'=4,'gy'=4,'gz'=2] {'gx'}, use_global_device_ids=true, to_apply=%region_20.0 | all-reduce | flops 2 | bytes 16 | tf_op jit(solution)/shard_map/psum | solution.py:127
  (1050 shorter events, 282.9 us)
Async XLA Ops:
  1.4 8.2 %collective-permute-start = (f32[1,32,128]{2,0,1:T(1,128)S(1)}, f32[1,32,128]{2,0,1:T(1,128)S(1)}, u32[]{:S(2)}, u32[]{:S(2)}) collective-permute-start(f32[1,32,128]{2,0,1:T(1,128)S(1)} %bitcast.399), channel_id=1, source_target_pairs={{8,0},{16,8},{24,16},{9,1},{17,9},{25,17},{10,2},{18,10},{26,18},{... | collective-permute-start | bytes 49160 | tf_op jit(solution)/shard_map/ppermute | solution.py:26
  2.7 7.0 %collective-permute-start.1 = (f32[1,32,128]{2,0,1:T(1,128)S(1)}, f32[1,32,128]{2,0,1:T(1,128)S(1)}, u32[]{:S(2)}, u32[]{:S(2)}) collective-permute-start(f32[1,32,128]{2,0,1:T(1,128)S(1)} %bitcast.398), channel_id=1, source_target_pairs={{0,8},{8,16},{16,24},{1,9},{9,17},{17,25},{2,10},{10,18},{18,26},{... | collective-permute-start | bytes 49160 | tf_op jit(solution)/shard_map/ppermute | solution.py:25
  15.5 6.2 %collective-permute-start.4 = (f32[34,34,1]{1,2,0:T(1,128)S(1)}, f32[34,34,1]{1,2,0:T(1,128)S(1)}, u32[]{:S(2)}, u32[]{:S(2)}) collective-permute-start(f32[34,34,1]{1,2,0:T(1,128)S(1)} %copy.400), channel_id=1, source_target_pairs={{1,0},{3,2},{5,4},{7,6},{9,8},{11,10},{13,12},{15,14},{17,16},{19,... | collective-permute-start | bytes 13880 | tf_op jit(solution)/shard_map/ppermute | solution.py:26
  17.2 6.0 %collective-permute-start.5 = (f32[34,34,1]{1,2,0:T(1,128)S(1)}, f32[34,34,1]{1,2,0:T(1,128)S(1)}, u32[]{:S(2)}, u32[]{:S(2)}) collective-permute-start(f32[34,34,1]{1,2,0:T(1,128)S(1)} %copy.402), channel_id=1, source_target_pairs={{0,1},{2,3},{4,5},{6,7},{8,9},{10,11},{12,13},{14,15},{16,17},{18,... | collective-permute-start | bytes 13880 | tf_op jit(solution)/shard_map/ppermute | solution.py:25
  82.3 5.9 %collective-permute-start.7 = (f32[5460]{0:T(1024)S(1)}, f32[5460]{0:T(1024)S(1)}, u32[]{:S(2)}, u32[]{:S(2)}) collective-permute-start(f32[5460]{0:T(1024)S(1)} %concatenate.1020), channel_id=1, source_target_pairs={{0,8},{8,16},{16,24},{1,9},{9,17},{17,25},{2,10},{10,18},{18,26},{... | collective-permute-start | bytes 65528 | tf_op jit(solution)/shard_map/ppermute | solution.py:15
  95.9 7.1 %collective-permute-start.8 = (f32[5964]{0:T(1024)S(1)}, f32[5964]{0:T(1024)S(1)}, u32[]{:S(2)}, u32[]{:S(2)}) collective-permute-start(f32[5964]{0:T(1024)S(1)} %concatenate.1027), channel_id=1, source_target_pairs={{2,0},{4,2},{6,4},{3,1},{5,3},{7,5},{10,8},{12,10},{14,12},{11,9},... | collective-permute-start | bytes 71576 | tf_op jit(solution)/shard_map/ppermute | solution.py:15
  106.6 7.2 %collective-permute-start.10 = (f32[1641]{0:T(1024)S(1)}, f32[1641]{0:T(1024)S(1)}, u32[]{:S(2)}, u32[]{:S(2)}) collective-permute-start(f32[1641]{0:T(1024)S(1)} %concatenate.1035), channel_id=1, source_target_pairs={{1,0},{3,2},{5,4},{7,6},{9,8},{11,10},{13,12},{15,14},{17,16},{19,... | collective-permute-start | bytes 19700 | tf_op jit(solution)/shard_map/ppermute | solution.py:15
  109.0 5.9 %collective-permute-start.11 = (f32[1641]{0:T(1024)S(1)}, f32[1641]{0:T(1024)S(1)}, u32[]{:S(2)}, u32[]{:S(2)}) collective-permute-start(f32[1641]{0:T(1024)S(1)} %concatenate.1037), channel_id=1, source_target_pairs={{0,1},{2,3},{4,5},{6,7},{8,9},{10,11},{12,13},{14,15},{16,17},{18,... | collective-permute-start | bytes 19700 | tf_op jit(solution)/shard_map/ppermute | solution.py:15
  145.3 7.0 %collective-permute-start.16 = (f32[1641]{0:T(1024)S(1)}, f32[1641]{0:T(1024)S(1)}, u32[]{:S(2)}, u32[]{:S(2)}) collective-permute-start(f32[1641]{0:T(1024)S(1)} %concatenate.1085), channel_id=1, source_target_pairs={{1,0},{3,2},{5,4},{7,6},{9,8},{11,10},{13,12},{15,14},{17,16},{19,... | collective-permute-start | bytes 19700 | tf_op jit(solution)/shard_map/ppermute | solution.py:15
  147.7 5.9 %collective-permute-start.17 = (f32[1641]{0:T(1024)S(1)}, f32[1641]{0:T(1024)S(1)}, u32[]{:S(2)}, u32[]{:S(2)}) collective-permute-start(f32[1641]{0:T(1024)S(1)} %concatenate.1087), channel_id=1, source_target_pairs={{0,1},{2,3},{4,5},{6,7},{8,9},{10,11},{12,13},{14,15},{16,17},{18,... | collective-permute-start | bytes 19700 | tf_op jit(solution)/shard_map/ppermute | solution.py:15
  163.2 7.2 %collective-permute-start.19 = (f32[5460]{0:T(1024)S(1)}, f32[5460]{0:T(1024)S(1)}, u32[]{:S(2)}, u32[]{:S(2)}) collective-permute-start(f32[5460]{0:T(1024)S(1)} %concatenate.1120), channel_id=1, source_target_pairs={{0,8},{8,16},{16,24},{1,9},{9,17},{17,25},{2,10},{10,18},{18,26},{... | collective-permute-start | bytes 65528 | tf_op jit(solution)/shard_map/ppermute | solution.py:15
  187.7 7.4 %collective-permute-start.22 = (f32[1641]{0:T(1024)S(1)}, f32[1641]{0:T(1024)S(1)}, u32[]{:S(2)}, u32[]{:S(2)}) collective-permute-start(f32[1641]{0:T(1024)S(1)} %concatenate.1135), channel_id=1, source_target_pairs={{1,0},{3,2},{5,4},{7,6},{9,8},{11,10},{13,12},{15,14},{17,16},{19,... | collective-permute-start | bytes 19700 | tf_op jit(solution)/shard_map/ppermute | solution.py:15
  190.2 5.9 %collective-permute-start.23 = (f32[1641]{0:T(1024)S(1)}, f32[1641]{0:T(1024)S(1)}, u32[]{:S(2)}, u32[]{:S(2)}) collective-permute-start(f32[1641]{0:T(1024)S(1)} %concatenate.1137), channel_id=1, source_target_pairs={{0,1},{2,3},{4,5},{6,7},{8,9},{10,11},{12,13},{14,15},{16,17},{18,... | collective-permute-start | bytes 19700 | tf_op jit(solution)/shard_map/ppermute | solution.py:15
  250.0 6.0 %collective-permute-start.25 = (f32[1,32,128]{2,0,1:T(1,128)S(1)}, f32[1,32,128]{2,0,1:T(1,128)S(1)}, u32[]{:S(2)}, u32[]{:S(2)}) collective-permute-start(f32[1,32,128]{2,0,1:T(1,128)S(1)} %get-tuple-element.152), channel_id=1, source_target_pairs={{0,8},{8,16},{16,24},{1,9},{9,17},{17,25},{2,10},{10,18},{18,26},{... | collective-permute-start | bytes 49160 | tf_op jit(solution)/shard_map/ppermute | solution.py:25
  261.8 6.2 %collective-permute-start.28 = (f32[34,34,1]{1,2,0:T(1,128)S(1)}, f32[34,34,1]{1,2,0:T(1,128)S(1)}, u32[]{:S(2)}, u32[]{:S(2)}) collective-permute-start(f32[34,34,1]{1,2,0:T(1,128)S(1)} %copy.506), channel_id=1, source_target_pairs={{1,0},{3,2},{5,4},{7,6},{9,8},{11,10},{13,12},{15,14},{17,16},{19,... | collective-permute-start | bytes 13880 | tf_op jit(solution)/shard_map/ppermute | solution.py:26
  263.5 6.0 %collective-permute-start.29 = (f32[34,34,1]{1,2,0:T(1,128)S(1)}, f32[34,34,1]{1,2,0:T(1,128)S(1)}, u32[]{:S(2)}, u32[]{:S(2)}) collective-permute-start(f32[34,34,1]{1,2,0:T(1,128)S(1)} %copy.508), channel_id=1, source_target_pairs={{0,1},{2,3},{4,5},{6,7},{8,9},{10,11},{12,13},{14,15},{16,17},{18,... | collective-permute-start | bytes 13880 | tf_op jit(solution)/shard_map/ppermute | solution.py:25
  379.9 7.0 %collective-permute-start.34 = (f32[1641]{0:T(1024)S(1)}, f32[1641]{0:T(1024)S(1)}, u32[]{:S(2)}, u32[]{:S(2)}) collective-permute-start(f32[1641]{0:T(1024)S(1)} %concatenate.1193), channel_id=1, source_target_pairs={{1,0},{3,2},{5,4},{7,6},{9,8},{11,10},{13,12},{15,14},{17,16},{19,... | collective-permute-start | bytes 19700 | tf_op jit(solution)/shard_map/ppermute | solution.py:15
  417.9 7.2 %collective-permute-start.40 = (f32[1641]{0:T(1024)S(1)}, f32[1641]{0:T(1024)S(1)}, u32[]{:S(2)}, u32[]{:S(2)}) collective-permute-start(f32[1641]{0:T(1024)S(1)} %concatenate.1243), channel_id=1, source_target_pairs={{1,0},{3,2},{5,4},{7,6},{9,8},{11,10},{13,12},{15,14},{17,16},{19,... | collective-permute-start | bytes 19700 | tf_op jit(solution)/shard_map/ppermute | solution.py:15
  420.5 5.9 %collective-permute-start.41 = (f32[1641]{0:T(1024)S(1)}, f32[1641]{0:T(1024)S(1)}, u32[]{:S(2)}, u32[]{:S(2)}) collective-permute-start(f32[1641]{0:T(1024)S(1)} %concatenate.1245), channel_id=1, source_target_pairs={{0,1},{2,3},{4,5},{6,7},{8,9},{10,11},{12,13},{14,15},{16,17},{18,... | collective-permute-start | bytes 19700 | tf_op jit(solution)/shard_map/ppermute | solution.py:15
  456.3 7.0 %collective-permute-start.46 = (f32[1641]{0:T(1024)S(1)}, f32[1641]{0:T(1024)S(1)}, u32[]{:S(2)}, u32[]{:S(2)}) collective-permute-start(f32[1641]{0:T(1024)S(1)} %concatenate.1293), channel_id=1, source_target_pairs={{1,0},{3,2},{5,4},{7,6},{9,8},{11,10},{13,12},{15,14},{17,16},{19,... | collective-permute-start | bytes 19700 | tf_op jit(solution)/shard_map/ppermute | solution.py:15
  458.7 5.9 %collective-permute-start.47 = (f32[1641]{0:T(1024)S(1)}, f32[1641]{0:T(1024)S(1)}, u32[]{:S(2)}, u32[]{:S(2)}) collective-permute-start(f32[1641]{0:T(1024)S(1)} %concatenate.1295), channel_id=1, source_target_pairs={{0,1},{2,3},{4,5},{6,7},{8,9},{10,11},{12,13},{14,15},{16,17},{18,... | collective-permute-start | bytes 19700 | tf_op jit(solution)/shard_map/ppermute | solution.py:15
  515.3 6.0 %collective-permute-start.49 = (f32[1,32,128]{2,0,1:T(1,128)S(1)}, f32[1,32,128]{2,0,1:T(1,128)S(1)}, u32[]{:S(2)}, u32[]{:S(2)}) collective-permute-start(f32[1,32,128]{2,0,1:T(1,128)S(1)} %get-tuple-element.144), channel_id=1, source_target_pairs={{0,8},{8,16},{16,24},{1,9},{9,17},{17,25},{2,10},{10,18},{18,26},{... | collective-permute-start | bytes 49160 | tf_op jit(solution)/shard_map/ppermute | solution.py:25
  527.8 6.2 %collective-permute-start.52 = (f32[34,34,1]{1,2,0:T(1,128)S(1)}, f32[34,34,1]{1,2,0:T(1,128)S(1)}, u32[]{:S(2)}, u32[]{:S(2)}) collective-permute-start(f32[34,34,1]{1,2,0:T(1,128)S(1)} %copy.612), channel_id=1, source_target_pairs={{1,0},{3,2},{5,4},{7,6},{9,8},{11,10},{13,12},{15,14},{17,16},{19,... | collective-permute-start | bytes 13880 | tf_op jit(solution)/shard_map/ppermute | solution.py:26
  529.4 6.0 %collective-permute-start.53 = (f32[34,34,1]{1,2,0:T(1,128)S(1)}, f32[34,34,1]{1,2,0:T(1,128)S(1)}, u32[]{:S(2)}, u32[]{:S(2)}) collective-permute-start(f32[34,34,1]{1,2,0:T(1,128)S(1)} %copy.614), channel_id=1, source_target_pairs={{0,1},{2,3},{4,5},{6,7},{8,9},{10,11},{12,13},{14,15},{16,17},{18,... | collective-permute-start | bytes 13880 | tf_op jit(solution)/shard_map/ppermute | solution.py:25
  (55 other events, 587.9 us)
